TPU v7x, 32 devices: a whole 2x2x4 slice. The times are simulated.
32 devices in a mesh: rows: 4 (over z), cols: 8 (over y, x, core).
Axes of the slice: x: 2, y: 2, z: 4, core: 2. Of those that a mesh axis runs over, the one named last changes fastest.
Arguments:
- features: bfloat16 [65536, 440], P(('rows', 'cols')), may hold values from -12 to 12
- residual: float32 [65536, 147], P(('rows', 'cols')), may hold values from -6 to 6
- coeffs: float32 [65536, 147], P(('rows', 'cols')), may hold values from -3 to 3
- block_inverse: float32 [2, 2048, 2048], P(None, ('rows', 'cols')), may hold values from -0.0234375 to 0.0234375
- block_index: int32 [2, 2048], P(None, 'cols'), may hold values from 0 to 2047, as said below
- owners: int32 [2], replicated, may hold values from 0 to 3
Outputs:
- new_coeffs: float32 [65536, 147], P(('rows', 'cols'))
- new_residual: float32 [65536, 147], P(('rows', 'cols'))
Inputs may be any that keep to these rules, and one draw needn't show every extreme that they name: `block_index`: for each step and each aligned run of 256 positions, the indices are distinct.
All inputs are finite; a program needn't handle non-finite values.
Results may differ from a plain program's by a relative error of at most 0.0028.
Values may be sent and summed in bfloat16 or wider, within the bound.
No kernel may reach another device: no remote copies, remote signals or barrier semaphores. Data moves between devices by JAX's collectives and lax.ppermute only.
A program may use at most 64 MiB of HBM per device.

v0:
```python
import jax
import jax.numpy as jnp
from jax import lax
from jax.sharding import PartitionSpec as P

penalty = 0.5


def from_root(value, axis, source):
    kept = jnp.where(lax.axis_index(axis) == source, value, 0).astype(value.dtype)
    return lax.psum(kept, axis)


def per_device(features, residual, coeffs, block_inverse, block_index, owners):
    frame_count = features.shape[0]
    feature_width = features.shape[1]
    per_col = block_index.shape[1]
    row_block = min(512, frame_count)
    exponent = -1.0 / feature_width
    my_row = lax.axis_index("rows")
    my_col = lax.axis_index("cols")
    squares = jnp.sum(jnp.square(features.astype(jnp.float32)), axis=1)
    feature_blocks = features.reshape(frame_count // row_block, row_block, feature_width)
    norm_blocks = squares.reshape(frame_count // row_block, row_block)
    for step_id in range(block_index.shape[0]):
        chosen_rows = block_index[step_id]
        owner_row = owners[step_id]
        mine_feat = jnp.take(features, chosen_rows, axis=0)
        mine_res = jnp.take(residual, chosen_rows, axis=0)
        row_piece = from_root(mine_feat, "rows", owner_row)
        chosen = lax.all_gather(row_piece, "cols", axis=0, tiled=True)
        res_piece = from_root(mine_res, "rows", owner_row)
        picked_res = lax.all_gather(res_piece, "cols", axis=0, tiled=True)
        my_update = jnp.dot(
            block_inverse[step_id],
            picked_res,
            precision=lax.Precision.HIGHEST,
            preferred_element_type=jnp.float32,
        ).astype(jnp.bfloat16)
        update = lax.all_gather(my_update, ("rows", "cols"), axis=0, tiled=True)
        chosen_norms = jnp.sum(jnp.square(chosen.astype(jnp.float32)), axis=1)

        def kernel_rows(operands):
            block_rows, block_norms = operands
            inner = lax.dot_general(
                block_rows, chosen, (((1,), (1,)), ((), ())), preferred_element_type=jnp.float32
            )
            distance = block_norms[:, None] + chosen_norms[None, :] - 2.0 * inner
            kernel = jnp.exp(distance * exponent).astype(jnp.bfloat16)
            return jnp.dot(kernel, update, preferred_element_type=jnp.float32)

        change = lax.map(kernel_rows, (feature_blocks, norm_blocks)).reshape(frame_count, -1)
        residual = residual - change
        is_owner = jnp.where(my_row == owner_row, 1.0, 0.0).astype(jnp.float32)
        mine_update = (
            lax.dynamic_slice_in_dim(update, my_col * per_col, per_col, 0).astype(jnp.float32)
            * is_owner
        )
        residual = residual.at[chosen_rows].add(-penalty * mine_update)
        coeffs = coeffs.at[chosen_rows].add(mine_update)
    return (coeffs, residual)


def solution(mesh):
    in_specs = (
        P(("rows", "cols"), None),
        P(("rows", "cols"), None),
        P(("rows", "cols"), None),
        P(None, ("rows", "cols"), None),
        P(None, "cols"),
        P(),
    )
    out_specs = (P(("rows", "cols"), None), P(("rows", "cols"), None))
    return jax.shard_map(
        per_device, mesh=mesh, in_specs=in_specs, out_specs=out_specs, check_vma=False
    )
```

profile of v0, /device:TPU:0, one launch (start us, length us, event | category | flops | bytes accessed | tf_op | source)
XLA Modules:
  0.0 380.8 jit_solution(9416683391688885127)
XLA Ops:
  7.2 0.8 fusion.40
  8.0 1.3 fusion.41
  9.3 1.8 copy.16
  11.8 1.0 gather_fusion
  12.7 0.8 select_select_fusion.3
  13.6 3.8 %copy.18 = bf16[2048,440]{1,0:T(8,128)(2,1)} copy(bf16[2048,440]{0,1:T(8,128)(2,1)} %param.14) | data formatting | bytes 3604480 | tf_op args[0]
  17.5 3.1 gather_fusion.1
  20.6 3.2 gather_fusion.3
  24.6 0.9 select_select_fusion
  25.6 26.5 %all-reduce.5.cloned.1.call-done = f32[256,147]{1,0:T(8,128)} async-done(((f32[256,147]{1,0:T(8,128)}), f32[256,147]{1,0:T(8,128)}) %all-reduce.5.cloned.1.call-update) | async-done | bytes 150544 | tf_op jit(solution)/shard_map/psum | solution.py:11
  52.1 41.4 %all-reduce.9.cloned.1.call-done = (bf16[256,440]{1,0:T(8,128)(2,1)}, bf16[256,440]{1,0:T(8,128)(2,1)}) async-done(((bf16[256,440]{1,0:T(8,128)(2,1)}, bf16[256,440]{1,0:T(8,128)(2,1)}), (bf16[256,440]{1,0:T(8,128)(2,1)}, bf16[256,440]{1,0:T(8,128)(2,1)})) %all-reduce.9.cloned.1.call-update) | async-done | bytes 450576 | tf_op jit(solution)/shard_map/psum | solution.py:11
  93.6 0.4 multiply_reduce_fusion.2
  94.0 29.0 %all-gather.5.cloned.1.call-done = f32[2048,147]{1,0:T(8,128)} async-done(((f32[256,147]{1,0:T(8,128)}), f32[2048,147]{1,0:T(8,128)}) %all-gather.5.cloned.1.call-update) | async-done | bytes 1204240 | tf_op jit(solution)/shard_map/all_gather | solution.py:33
  123.1 2.9 fusion.18
  126.0 46.2 %all_gather.19 = bf16[2048,147]{1,0:T(8,128)(2,1)} all-gather(bf16[64,147]{1,0:T(8,128)(2,1)S(1)} %fusion.18), channel_id=1, replica_groups=mesh['rows'=4,'cols'=8] {'rows','cols'}, dimensions={0}, use_global_device_ids=true | all-gather | bytes 620928 | tf_op jit(solution)/shard_map/all_gather | solution.py:40
  172.2 2.3 multiply_reduce_fusion.1
  174.4 0.1 broadcast.62.clone
  174.6 14.1 %while.20 = (s32[]{:T(128)}, f32[4,512,147]{1,2,0:T(8,128)S(1)}, f32[4,512]{1,0:T(4,128)S(1)}, f32[2048]{0:T(1024)S(1)}, bf16[4,512,440]{2,1,0:T(8,128)(2,1)}, /...) while((s32[]{:T(128)}, f32[4,512,147]{1,2,0:T(8,128)S(1)}, f32[4,512]{1,0:T(4,128)S(1)}, ...), condition=%wide.region_6.9_spmd, body=%wide.region_5.8_spmd.sunk | while | flops 1236271104 | bytes 3996761 | solution.py:52
  174.6 3.5 fusion.59
  178.2 3.5 fusion.59
  181.7 3.5 fusion.59
  185.2 3.5 fusion.59
  188.7 1.8 copy.20
  190.5 2.5 bitcast_subtract_fusion.1
  193.0 3.1 scatter_custom_fusion.1
  196.1 1.7 gather_fusion.2
  197.8 1.8 select_select_fusion.1
  199.6 0.5 all-gather.11.cloned.1.call-update
  200.2 0.2 all-gather.9.cloned.1.call-start
  200.4 31.0 %all-reduce.7.cloned.1.call-done = f32[256,147]{1,0:T(8,128)} async-done(((f32[256,147]{1,0:T(8,128)}), f32[256,147]{1,0:T(8,128)}) %all-reduce.7.cloned.1.call-update) | async-done | bytes 150544 | tf_op jit(solution)/shard_map/psum | solution.py:11
  231.5 1.8 copy.17
  233.3 5.2 %scatter_custom_fusion = f32[2048,147]{1,0:T(8,128)} fusion(f32[2048,147]{1,0:T(8,128)} %copy.17, s32[256]{0:T(256)S(1)} %bitcast.79, f32[]{:T(128)S(6)} %select_n.78, bf16[2048,147]{1,0:T(8,128)(2,1)} %get-tuple-element.271, s32[]{:T(128)S(6)} %select_n.77, s32[]{:T(128)} %constant.43.clone.1), kind=kCustom, calls=%fused_computation.50 | custom fusion | flops 112896 | bytes 1335816 | tf_op jit(solution)/shard_map/scatter-add | solution.py:60
  238.5 22.4 %all-gather.11.cloned.1.call-done = bf16[2048,440]{1,0:T(8,128)(2,1)} async-done(((bf16[256,440]{1,0:T(8,128)(2,1)}), bf16[2048,440]{1,0:T(8,128)(2,1)}) %all-gather.11.cloned.1.call-update) | async-done | bytes 1802256 | tf_op jit(solution)/shard_map/all_gather | solution.py:31
  260.9 2.1 multiply_reduce_fusion
  263.0 27.6 %all-gather.9.cloned.1.call-done = f32[2048,147]{1,0:T(8,128)} async-done(((f32[256,147]{1,0:T(8,128)}), f32[2048,147]{1,0:T(8,128)}) %all-gather.9.cloned.1.call-update) | async-done | bytes 1204240 | tf_op jit(solution)/shard_map/all_gather | solution.py:33
  290.6 2.9 fusion.19
  293.5 46.1 %all_gather.22 = bf16[2048,147]{1,0:T(8,128)(2,1)} all-gather(bf16[64,147]{1,0:T(8,128)(2,1)S(1)} %fusion.19), channel_id=1, replica_groups=mesh['rows'=4,'cols'=8] {'rows','cols'}, dimensions={0}, use_global_device_ids=true | all-gather | bytes 620928 | tf_op jit(solution)/shard_map/all_gather | solution.py:40
  339.7 16.6 %while.21 = (s32[]{:T(128)}, f32[4,512,147]{1,2,0:T(8,128)S(1)}, f32[4,512]{1,0:T(4,128)S(1)}, f32[2048]{0:T(1024)S(1)}, bf16[4,512,440]{2,1,0:T(8,128)(2,1)}, /...) while((s32[]{:T(128)}, f32[4,512,147]{1,2,0:T(8,128)S(1)}, f32[4,512]{1,0:T(4,128)S(1)}, ...), condition=%wide.region_13.16_spmd, body=%wide.region_12.15_spmd.sunk | while | flops 1236271104 | bytes 3996761 | solution.py:52
  339.7 4.1 %fusion.63 = f32[4,512,147]{1,2,0:T(8,128)S(1)} fusion(f32[4,512,147]{1,2,0:T(8,128)S(1)} %get-tuple-element.241, s32[]{:T(128)} %get-tuple-element.240, bf16[2048,147]{1,0:T(8,128)(2,1)} %get-tuple-element.254, bf16[2048,440]{1,0:T(8,128)(2,1)} %get-tuple-element.253, f32[2048]{0:T(1024)S(1)} %get-tuple-element.251, f32[512]{0:T(512)S(1)} %bitcast.71, ...), kind=kOutput, calls=%fused_computation.19.clone.1 | convolution fusion | flops 1236271104 | bytes 3992576 | tf_op jit(solution)/shard_map/while/body/eval_jaxpr/dot_general | solution.py:50
  343.9 4.1 %fusion.63 = f32[4,512,147]{1,2,0:T(8,128)S(1)} fusion(f32[4,512,147]{1,2,0:T(8,128)S(1)} %get-tuple-element.241, s32[]{:T(128)} %get-tuple-element.240, bf16[2048,147]{1,0:T(8,128)(2,1)} %get-tuple-element.254, bf16[2048,440]{1,0:T(8,128)(2,1)} %get-tuple-element.253, f32[2048]{0:T(1024)S(1)} %get-tuple-element.251, f32[512]{0:T(512)S(1)} %bitcast.71, ...), kind=kOutput, calls=%fused_computation.19.clone.1 | convolution fusion | flops 1236271104 | bytes 3992576 | tf_op jit(solution)/shard_map/while/body/eval_jaxpr/dot_general | solution.py:50
  348.1 4.1 %fusion.63 = f32[4,512,147]{1,2,0:T(8,128)S(1)} fusion(f32[4,512,147]{1,2,0:T(8,128)S(1)} %get-tuple-element.241, s32[]{:T(128)} %get-tuple-element.240, bf16[2048,147]{1,0:T(8,128)(2,1)} %get-tuple-element.254, bf16[2048,440]{1,0:T(8,128)(2,1)} %get-tuple-element.253, f32[2048]{0:T(1024)S(1)} %get-tuple-element.251, f32[512]{0:T(512)S(1)} %bitcast.71, ...), kind=kOutput, calls=%fused_computation.19.clone.1 | convolution fusion | flops 1236271104 | bytes 3992576 | tf_op jit(solution)/shard_map/while/body/eval_jaxpr/dot_general | solution.py:50
  352.2 4.1 %fusion.63 = f32[4,512,147]{1,2,0:T(8,128)S(1)} fusion(f32[4,512,147]{1,2,0:T(8,128)S(1)} %get-tuple-element.241, s32[]{:T(128)} %get-tuple-element.240, bf16[2048,147]{1,0:T(8,128)(2,1)} %get-tuple-element.254, bf16[2048,440]{1,0:T(8,128)(2,1)} %get-tuple-element.253, f32[2048]{0:T(1024)S(1)} %get-tuple-element.251, f32[512]{0:T(512)S(1)} %bitcast.71, ...), kind=kOutput, calls=%fused_computation.19.clone.1 | convolution fusion | flops 1236271104 | bytes 3992576 | tf_op jit(solution)/shard_map/while/body/eval_jaxpr/dot_general | solution.py:50
  356.3 1.8 copy.23
  358.1 3.2 bitcast_subtract_fusion
  361.3 5.1 %scatter_custom_fusion.3 = f32[2048,147]{1,0:T(8,128)} fusion(f32[2048,147]{1,0:T(8,128)} %bitcast_subtract_fusion, s32[256]{0:T(256)S(1)} %bitcast.76, f32[]{:T(128)S(6)} %select_n.84, f32[]{:T(128)} %constant.72.clone.1, bf16[2048,147]{1,0:T(8,128)(2,1)} %get-tuple-element.272, s32[]{:T(128)S(6)} %select_n.77, s32[]{:T(128)} %constant.43.clone.1), kind=kCustom, calls=%fused_computation.43 | custom fusion | flops 150528 | bytes 1336328 | tf_op jit(solution)/shard_map/scatter-add | solution.py:59
  366.4 2.8 copy.25
  369.2 3.1 scatter_custom_fusion.2
  372.4 1.6 copy.24
  (46 shorter events, 0.6 us)
Async XLA Ops:
  7.2 44.9 %all-reduce.5.cloned.1.call-start = ((), (), s32[]{:S(2)}) async-start(), calls=%async_computation | async-start | bytes 524288 | tf_op jit(solution)/shard_map/psum | solution.py:11
  11.1 6.4 %copy-start = (f32[2048,147]{1,0:T(8,128)}, f32[2048,147]{1,0:T(8,128)S(1)}, u32[]{:S(2)}) copy-start(f32[2048,147]{1,0:T(8,128)S(1)} %copy.16) | copy-start | bytes 3612676
  13.6 80.0 %all-reduce.9.cloned.1.call-start = ((), (), s32[]{:S(2)}) async-start(), calls=%async_computation.6 | async-start | bytes 1048576 | tf_op jit(solution)/shard_map/psum | solution.py:11
  20.5 73.1 %copy-start.2 = (bf16[2048,440]{0,1:T(8,128)(2,1)S(1)}, bf16[2048,440]{0,1:T(8,128)(2,1)}, u32[]{:S(2)}) copy-start(bf16[2048,440]{0,1:T(8,128)(2,1)} %param.14) | copy-start | bytes 5406724
  23.8 70.2 %copy-start.7 = (s32[2,256]{1,0:T(2,128)S(1)}, s32[2,256]{1,0:T(2,128)}, u32[]{:S(2)}) copy-start(s32[2,256]{1,0:T(2,128)} %param.18) | copy-start | bytes 6148
  23.8 99.3 %copy-start.5 = (f32[2,64,2048]{2,1,0:T(8,128)S(1)}, f32[2,64,2048]{2,1,0:T(8,128)}, u32[]{:S(2)}) copy-start(f32[2,64,2048]{2,1,0:T(8,128)} %param.17) | copy-start | bytes 3145732
  25.5 97.5 %all-gather.5.cloned.1.call-start = ((), (), s32[]{:S(2)}) async-start(), calls=%async_computation.1 | async-start | bytes 2359296 | tf_op jit(solution)/shard_map/all_gather | solution.py:33
  52.1 120.1 %all-gather.7.cloned.1.call-start = ((), (), s32[]{:S(2)}) async-start(), calls=%async_computation.2 | async-start | bytes 2359296 | tf_op jit(solution)/shard_map/all_gather | solution.py:31
  93.6 137.9 %all-reduce.7.cloned.1.call-start = ((), (), s32[]{:S(2)}) async-start(), calls=%async_computation.3 | async-start | bytes 524288 | tf_op jit(solution)/shard_map/psum | solution.py:11
  172.2 2.4 copy-start.3
  196.1 35.3 %copy-start.4 = (f32[2048,147]{0,1:T(8,128)S(1)}, f32[2048,147]{0,1:T(8,128)}, u32[]{:S(2)}) copy-start(f32[2048,147]{0,1:T(8,128)} %param.16) | copy-start | bytes 3612676
  199.6 61.3 %all-gather.11.cloned.1.call-start = ((), (), s32[]{:S(2)}) async-start(), calls=%async_computation.5 | async-start | bytes 2359296 | tf_op jit(solution)/shard_map/all_gather | solution.py:31
  200.2 90.4 %all-gather.9.cloned.1.call-start = ((), (), s32[]{:S(2)}) async-start(), calls=%async_computation.4 | async-start | bytes 2359296 | tf_op jit(solution)/shard_map/all_gather | solution.py:33
  233.3 57.3 %copy-start.6 = (f32[2,64,2048]{2,1,0:T(8,128)S(1)}, f32[2,64,2048]{2,1,0:T(8,128)}, u32[]{:S(2)}) copy-start(f32[2,64,2048]{2,1,0:T(8,128)} %param.17) | copy-start | bytes 3145732
  366.4 2.8 copy-start.1
Sparse Core Ops, SparseCore 0:
  13.7 38.3 all-reduce.4
  55.0 38.4 all-reduce.8
  95.4 27.5 all-gather.4
  124.8 31.5 all-gather.6
  199.7 31.6 all-reduce.6
  233.2 27.6 all-gather.10
  262.8 27.7 all-gather.8
where the time goes:
time: 382 us; the launch traced here: 381 us
  waiting for transfers between devices  179 us (47%)
  blocking collectives  92.3 us (24%)
  matrix products  36.3 us (10%)
  other arithmetic  30.5 us (8%)
  local copies, waits for them, and re-layouts  26.8 us (7%)
  between operations  15.7 us (4%)
    psum x3, waiting for transfers between devices, from_root(): return lax.psum(kept, axis)  98.9 us
    all_gather x2, blocking collectives, per_device(): update = lax.all_gather(my_update, ('rows', 'cols'), axis=0, tiled=True)  92.3 us
    all_gather x2, waiting for transfers between devices, per_device(): picked_res = lax.all_gather(res_piece, 'cols', axis=0, tiled=True)  56.6 us
    dot_general x8, matrix products, kernel_rows(): return jnp.dot(kernel, update, preferred_element_type=jnp.float32)  30.5 us
    all_gather x2, waiting for transfers between devices, per_device(): chosen = lax.all_gather(row_piece, 'cols', axis=0, tiled=True)  22.4 us
    unnamed x21, local copies, waits for them, and re-layouts  11.9 us
    scatter-add x2, other arithmetic, per_device(): coeffs = coeffs.at[chosen_rows].add(mine_update)  8.29 us
    scatter-add x2, other arithmetic, per_device(): residual = residual.at[chosen_rows].add(-penalty * mine_update)  8.22 us
  transfers between devices with their start and end apart: 7, of which 6 were waited for; matrix products, arithmetic and copies ran while one was open for 6% of the time, Pallas kernels for 0%

commit v1 on v0

--- a/solution.py
+++ b/solution.py
@@ -8,7 +8,7 @@
 
 def from_root(value, axis, source):
     kept = jnp.where(lax.axis_index(axis) == source, value, 0).astype(value.dtype)
-    return lax.psum(kept, axis)
+    return jnp.sum(lax.all_gather(kept, axis), axis=0)
 
 
 def per_device(features, residual, coeffs, block_inverse, block_index, owners):

time: 382 us -> 306 us (0.80)
  waiting for transfers between devices: 179 us -> 14.5 us
  blocking collectives: 92.3 us -> 181 us
    psum x3 -> x0, waiting for transfers between devices: 98.9 us -> none  [from_root(): return lax.psum(kept, axis)]
    all_gather x0 -> x4, blocking collectives: none -> 88.2 us  [from_root(): return jnp.sum(lax.all_gather(kept, axis), axis=0)]
    all_gather x2, waiting for transfers between devices: 56.6 us -> 14.5 us  [per_device(): picked_res = lax.all_gather(res_piece, 'cols', axis=0, tiled=True)]
    all_gather x2, waiting for transfers between devices: 22.4 us -> 0.01 us  [per_device(): chosen = lax.all_gather(row_piece, 'cols', axis=0, tiled=True)]
    gather x2, local copies, waits for them, and re-layouts: 6.32 us -> 2.31 us  [per_device(): mine_feat = jnp.take(features, chosen_rows, axis=0)]
    unnamed x21 -> x17, local copies, waits for them, and re-layouts: 11.9 us -> 13.1 us
  transfers between devices with their start and end apart: 7 -> 4, of which waited for: 6 -> 1; matrix products, arithmetic and copies ran while one was open for 6% -> 16% of each run, Pallas kernels for 0% -> 0%
where the time goes in v1:
time: 306 us; the launch traced here: 305 us
  blocking collectives  181 us (59%)
  matrix products  38 us (12%)
  other arithmetic  32.4 us (11%)
  local copies, waits for them, and re-layouts  23.4 us (8%)
  between operations  15.3 us (5%)
  waiting for transfers between devices  14.5 us (5%)
    all_gather x2, blocking collectives, per_device(): update = lax.all_gather(my_update, ('rows', 'cols'), axis=0, tiled=True)  92.5 us
    all_gather x4, blocking collectives, from_root(): return jnp.sum(lax.all_gather(kept, axis), axis=0)  88.2 us
    dot_general x8, matrix products, kernel_rows(): return jnp.dot(kernel, update, preferred_element_type=jnp.float32)  32.2 us
    all_gather x2, waiting for transfers between devices, per_device(): picked_res = lax.all_gather(res_piece, 'cols', axis=0, tiled=True)  14.5 us
    unnamed x17, local copies, waits for them, and re-layouts  13.1 us
    scatter-add x2, other arithmetic, per_device(): coeffs = coeffs.at[chosen_rows].add(mine_update)  8.37 us
    scatter-add x2, other arithmetic, per_device(): residual = residual.at[chosen_rows].add(-penalty * mine_update)  8.22 us
  transfers between devices with their start and end apart: 4, of which 1 were waited for; matrix products, arithmetic and copies ran while one was open for 16% of the time, Pallas kernels for 0%

profile of v1, /device:TPU:0, one launch (start us, length us, event | category | flops | bytes accessed | tf_op | source)
XLA Modules:
  0.0 304.8 jit_solution(15840975665185126270)
XLA Ops:
  7.2 0.8 fusion.40
  8.0 1.4 fusion.41
  9.4 1.8 copy.16
  11.8 1.0 gather_fusion
  12.9 24.2 %all-gather = f32[1024,147]{1,0:T(8,128)S(1)} all-gather(f32[256,147]{1,0:T(8,128)S(1)} %select_select_fusion.3), channel_id=2, replica_groups=mesh['rows'=4,'cols'=8] {'rows'}, dimensions={0}, use_global_device_ids=true | all-gather | bytes 752640 | tf_op jit(solution)/shard_map/all_gather | solution.py:11
  37.1 0.8 reduce_sum.69
  38.0 2.8 copy.18
  40.8 1.2 gather_fusion.1
  42.1 21.7 %all-gather.1 = bf16[1024,440]{1,0:T(8,128)(2,1)S(1)} all-gather(bf16[256,440]{1,0:T(8,128)(2,1)S(1)} %select_select_fusion.2), channel_id=3, replica_groups=mesh['rows'=4,'cols'=8] {'rows'}, dimensions={0}, use_global_device_ids=true | all-gather | bytes 1126400 | tf_op jit(solution)/shard_map/all_gather | solution.py:11
  63.8 0.9 reduce_sum.71
  65.5 1.2 gather_fusion.3
  66.8 20.2 %all-gather.3 = bf16[1024,440]{1,0:T(8,128)(2,1)S(1)} all-gather(bf16[256,440]{1,0:T(8,128)(2,1)S(1)} %select_select_fusion), channel_id=5, replica_groups=mesh['rows'=4,'cols'=8] {'rows'}, dimensions={0}, use_global_device_ids=true | all-gather | bytes 1126400 | tf_op jit(solution)/shard_map/all_gather | solution.py:11
  87.0 0.9 reduce_sum.74
  88.1 1.9 multiply_reduce_fusion.2
  90.1 2.9 fusion.18
  93.0 46.4 %all_gather.45 = bf16[2048,147]{1,0:T(8,128)(2,1)} all-gather(bf16[64,147]{1,0:T(8,128)(2,1)S(1)} %fusion.18), channel_id=1, replica_groups=mesh['rows'=4,'cols'=8] {'rows','cols'}, dimensions={0}, use_global_device_ids=true | all-gather | bytes 620928 | tf_op jit(solution)/shard_map/all_gather | solution.py:40
  139.4 2.1 multiply_reduce_fusion.1
  141.6 0.1 broadcast.62.clone
  141.7 15.9 %while.20 = (s32[]{:T(128)}, f32[4,512,147]{1,2,0:T(8,128)S(1)}, f32[4,512]{1,0:T(4,128)S(1)}, f32[2048]{0:T(1024)S(1)}, bf16[4,512,440]{2,1,0:T(8,128)(2,1)S(1)...) while((s32[]{:T(128)}, f32[4,512,147]{1,2,0:T(8,128)S(1)}, f32[4,512]{1,0:T(4,128)S(1)}, ...), condition=%wide.region_6.9_spmd, body=%wide.region_5.8_spmd.sunk | while | flops 1236271104 | bytes 3996761 | solution.py:52
  141.7 3.9 %fusion.59 = f32[4,512,147]{1,2,0:T(8,128)S(1)} fusion(f32[4,512,147]{1,2,0:T(8,128)S(1)} %get-tuple-element.213, s32[]{:T(128)} %get-tuple-element.212, bf16[2048,147]{1,0:T(8,128)(2,1)} %get-tuple-element.226, bf16[2048,440]{1,0:T(8,128)(2,1)} %get-tuple-element.225, f32[2048]{0:T(1024)S(1)} %get-tuple-element.223, f32[512]{0:T(512)S(1)} %bitcast.78, ...), kind=kOutput, calls=%fused_computation.10.clone.1 | convolution fusion | flops 1236271104 | bytes 3992576 | tf_op jit(solution)/shard_map/while/body/eval_jaxpr/dot_general | solution.py:50
  145.7 3.9 %fusion.59 = f32[4,512,147]{1,2,0:T(8,128)S(1)} fusion(f32[4,512,147]{1,2,0:T(8,128)S(1)} %get-tuple-element.213, s32[]{:T(128)} %get-tuple-element.212, bf16[2048,147]{1,0:T(8,128)(2,1)} %get-tuple-element.226, bf16[2048,440]{1,0:T(8,128)(2,1)} %get-tuple-element.225, f32[2048]{0:T(1024)S(1)} %get-tuple-element.223, f32[512]{0:T(512)S(1)} %bitcast.78, ...), kind=kOutput, calls=%fused_computation.10.clone.1 | convolution fusion | flops 1236271104 | bytes 3992576 | tf_op jit(solution)/shard_map/while/body/eval_jaxpr/dot_general | solution.py:50
  149.7 3.9 %fusion.59 = f32[4,512,147]{1,2,0:T(8,128)S(1)} fusion(f32[4,512,147]{1,2,0:T(8,128)S(1)} %get-tuple-element.213, s32[]{:T(128)} %get-tuple-element.212, bf16[2048,147]{1,0:T(8,128)(2,1)} %get-tuple-element.226, bf16[2048,440]{1,0:T(8,128)(2,1)} %get-tuple-element.225, f32[2048]{0:T(1024)S(1)} %get-tuple-element.223, f32[512]{0:T(512)S(1)} %bitcast.78, ...), kind=kOutput, calls=%fused_computation.10.clone.1 | convolution fusion | flops 1236271104 | bytes 3992576 | tf_op jit(solution)/shard_map/while/body/eval_jaxpr/dot_general | solution.py:50
  153.7 3.9 %fusion.59 = f32[4,512,147]{1,2,0:T(8,128)S(1)} fusion(f32[4,512,147]{1,2,0:T(8,128)S(1)} %get-tuple-element.213, s32[]{:T(128)} %get-tuple-element.212, bf16[2048,147]{1,0:T(8,128)(2,1)} %get-tuple-element.226, bf16[2048,440]{1,0:T(8,128)(2,1)} %get-tuple-element.225, f32[2048]{0:T(1024)S(1)} %get-tuple-element.223, f32[512]{0:T(512)S(1)} %bitcast.78, ...), kind=kOutput, calls=%fused_computation.10.clone.1 | convolution fusion | flops 1236271104 | bytes 3992576 | tf_op jit(solution)/shard_map/while/body/eval_jaxpr/dot_general | solution.py:50
  157.6 1.3 copy-done.1
  158.9 1.8 copy.20
  160.7 2.5 bitcast_subtract_fusion.1
  163.2 3.1 %scatter_custom_fusion.1 = f32[2048,147]{1,0:T(8,128)S(1)} fusion(f32[2048,147]{1,0:T(8,128)S(1)} %bitcast_subtract_fusion.1, s32[256]{0:T(256)S(1)} %bitcast.86, f32[]{:T(128)} %constant.74.clone.1, f32[]{:T(128)S(6)} %select_n.78, bf16[2048,147]{1,0:T(8,128)(2,1)} %get-tuple-element.261, s32[]{:T(128)S(6)} %select_n.77, s32[]{:T(128)} %constant.50.clone.1), kind=kCustom, calls=%fused_computation.47 | custom fusion | flops 150528 | bytes 1336328 | tf_op jit(solution)/shard_map/scatter-add | solution.py:59
  166.4 1.0 gather_fusion.2
  167.4 22.1 %all-gather.2 = f32[1024,147]{1,0:T(8,128)S(1)} all-gather(f32[256,147]{1,0:T(8,128)S(1)} %select_select_fusion.1), channel_id=4, replica_groups=mesh['rows'=4,'cols'=8] {'rows'}, dimensions={0}, use_global_device_ids=true | all-gather | bytes 752640 | tf_op jit(solution)/shard_map/all_gather | solution.py:11
  189.5 0.8 reduce_sum.73
  190.3 2.8 copy.17
  193.1 5.3 %scatter_custom_fusion = f32[2048,147]{1,0:T(8,128)} fusion(f32[2048,147]{1,0:T(8,128)} %copy.17, s32[256]{0:T(256)S(1)} %bitcast.87, f32[]{:T(128)S(6)} %select_n.78, bf16[2048,147]{1,0:T(8,128)(2,1)} %get-tuple-element.261, s32[]{:T(128)S(6)} %select_n.77, s32[]{:T(128)} %constant.50.clone.1), kind=kCustom, calls=%fused_computation.50 | custom fusion | flops 112896 | bytes 1335816 | tf_op jit(solution)/shard_map/scatter-add | solution.py:60
  198.4 2.1 multiply_reduce_fusion
  200.5 14.5 %all-gather.13.cloned.1.call-done = f32[2048,147]{1,0:T(8,128)} async-done(((f32[256,147]{1,0:T(8,128)}), f32[2048,147]{1,0:T(8,128)}) %all-gather.13.cloned.1.call-update) | async-done | bytes 1204240 | tf_op jit(solution)/shard_map/all_gather | solution.py:33
  214.9 2.9 fusion.19
  217.9 46.1 %all_gather.52 = bf16[2048,147]{1,0:T(8,128)(2,1)} all-gather(bf16[64,147]{1,0:T(8,128)(2,1)S(1)} %fusion.19), channel_id=1, replica_groups=mesh['rows'=4,'cols'=8] {'rows','cols'}, dimensions={0}, use_global_device_ids=true | all-gather | bytes 620928 | tf_op jit(solution)/shard_map/all_gather | solution.py:40
  263.9 0.1 broadcast.62
  264.1 16.6 %while.21 = (s32[]{:T(128)}, f32[4,512,147]{1,2,0:T(8,128)S(1)}, f32[4,512]{1,0:T(4,128)S(1)}, f32[2048]{0:T(1024)S(1)}, bf16[4,512,440]{2,1,0:T(8,128)(2,1)}, /...) while((s32[]{:T(128)}, f32[4,512,147]{1,2,0:T(8,128)S(1)}, f32[4,512]{1,0:T(4,128)S(1)}, ...), condition=%wide.region_13.16_spmd, body=%wide.region_12.15_spmd.sunk | while | flops 1236271104 | bytes 3996761 | solution.py:52
  264.1 4.1 %fusion.63 = f32[4,512,147]{1,2,0:T(8,128)S(1)} fusion(f32[4,512,147]{1,2,0:T(8,128)S(1)} %get-tuple-element.237, s32[]{:T(128)} %get-tuple-element.236, bf16[2048,147]{1,0:T(8,128)(2,1)} %get-tuple-element.250, bf16[2048,440]{1,0:T(8,128)(2,1)} %get-tuple-element.249, f32[2048]{0:T(1024)S(1)} %get-tuple-element.247, f32[512]{0:T(512)S(1)} %bitcast.79, ...), kind=kOutput, calls=%fused_computation.19.clone.1 | convolution fusion | flops 1236271104 | bytes 3992576 | tf_op jit(solution)/shard_map/while/body/eval_jaxpr/dot_general | solution.py:50
  268.3 4.1 %fusion.63 = f32[4,512,147]{1,2,0:T(8,128)S(1)} fusion(f32[4,512,147]{1,2,0:T(8,128)S(1)} %get-tuple-element.237, s32[]{:T(128)} %get-tuple-element.236, bf16[2048,147]{1,0:T(8,128)(2,1)} %get-tuple-element.250, bf16[2048,440]{1,0:T(8,128)(2,1)} %get-tuple-element.249, f32[2048]{0:T(1024)S(1)} %get-tuple-element.247, f32[512]{0:T(512)S(1)} %bitcast.79, ...), kind=kOutput, calls=%fused_computation.19.clone.1 | convolution fusion | flops 1236271104 | bytes 3992576 | tf_op jit(solution)/shard_map/while/body/eval_jaxpr/dot_general | solution.py:50
  272.4 4.1 %fusion.63 = f32[4,512,147]{1,2,0:T(8,128)S(1)} fusion(f32[4,512,147]{1,2,0:T(8,128)S(1)} %get-tuple-element.237, s32[]{:T(128)} %get-tuple-element.236, bf16[2048,147]{1,0:T(8,128)(2,1)} %get-tuple-element.250, bf16[2048,440]{1,0:T(8,128)(2,1)} %get-tuple-element.249, f32[2048]{0:T(1024)S(1)} %get-tuple-element.247, f32[512]{0:T(512)S(1)} %bitcast.79, ...), kind=kOutput, calls=%fused_computation.19.clone.1 | convolution fusion | flops 1236271104 | bytes 3992576 | tf_op jit(solution)/shard_map/while/body/eval_jaxpr/dot_general | solution.py:50
  276.5 4.1 %fusion.63 = f32[4,512,147]{1,2,0:T(8,128)S(1)} fusion(f32[4,512,147]{1,2,0:T(8,128)S(1)} %get-tuple-element.237, s32[]{:T(128)} %get-tuple-element.236, bf16[2048,147]{1,0:T(8,128)(2,1)} %get-tuple-element.250, bf16[2048,440]{1,0:T(8,128)(2,1)} %get-tuple-element.249, f32[2048]{0:T(1024)S(1)} %get-tuple-element.247, f32[512]{0:T(512)S(1)} %bitcast.79, ...), kind=kOutput, calls=%fused_computation.19.clone.1 | convolution fusion | flops 1236271104 | bytes 3992576 | tf_op jit(solution)/shard_map/while/body/eval_jaxpr/dot_general | solution.py:50
  280.7 1.8 copy.23
  282.4 3.2 %bitcast_subtract_fusion = f32[2048,147]{1,0:T(8,128)} fusion(f32[2048,147]{1,0:T(8,128)S(1)} %scatter_custom_fusion.1, f32[4,512,147]{2,1,0:T(8,128)} %copy.23), kind=kLoop, calls=%fused_computation.29 | loop fusion | flops 301056 | bytes 3612672 | tf_op jit(solution)/shard_map/sub | solution.py:53
  285.7 5.1 %scatter_custom_fusion.3 = f32[2048,147]{1,0:T(8,128)} fusion(f32[2048,147]{1,0:T(8,128)} %bitcast_subtract_fusion, s32[256]{0:T(256)S(1)} %bitcast.84, f32[]{:T(128)S(6)} %select_n.84, f32[]{:T(128)} %constant.74.clone.1, bf16[2048,147]{1,0:T(8,128)(2,1)} %get-tuple-element.262, s32[]{:T(128)S(6)} %select_n.77, s32[]{:T(128)} %constant.50.clone.1), kind=kCustom, calls=%fused_computation.43 | custom fusion | flops 150528 | bytes 1336328 | tf_op jit(solution)/shard_map/scatter-add | solution.py:59
  290.8 2.8 copy.25
  293.6 3.1 %scatter_custom_fusion.2 = f32[2048,147]{1,0:T(8,128)S(1)} fusion(f32[2048,147]{1,0:T(8,128)S(1)} %copy-done.2, s32[256]{0:T(256)S(1)} %bitcast.85, f32[]{:T(128)S(6)} %select_n.84, bf16[2048,147]{1,0:T(8,128)(2,1)} %get-tuple-element.262, s32[]{:T(128)S(6)} %select_n.77, s32[]{:T(128)} %constant.50.clone.1), kind=kCustom, calls=%fused_computation.46 | custom fusion | flops 112896 | bytes 1335816 | tf_op jit(solution)/shard_map/scatter-add | solution.py:60
  296.7 1.6 copy.24
  (42 shorter events, 0.8 us)
Async XLA Ops:
  7.2 82.9 %all-gather.9.cloned.1.call-start = ((), (), s32[]{:S(2)}) async-start(), calls=%async_computation | async-start | bytes 2359296 | tf_op jit(solution)/shard_map/all_gather | solution.py:33
  11.2 25.9 %copy-start = (f32[2048,147]{1,0:T(8,128)}, f32[2048,147]{1,0:T(8,128)S(1)}, u32[]{:S(2)}) copy-start(f32[2048,147]{1,0:T(8,128)S(1)} %copy.16) | copy-start | bytes 3612676
  37.9 101.5 %all-gather.11.cloned.1.call-start = ((), (), s32[]{:S(2)}) async-start(), calls=%async_computation.1 | async-start | bytes 2359296 | tf_op jit(solution)/shard_map/all_gather | solution.py:31
  64.7 133.6 %all-gather.15.cloned.1.call-start = ((), (), s32[]{:S(2)}) async-start(), calls=%async_computation.3 | async-start | bytes 2359296 | tf_op jit(solution)/shard_map/all_gather | solution.py:31
  66.8 23.2 %copy-start.5 = (s32[2,256]{1,0:T(2,128)S(1)}, s32[2,256]{1,0:T(2,128)}, u32[]{:S(2)}) copy-start(s32[2,256]{1,0:T(2,128)} %param.18) | copy-start | bytes 6148
  88.0 2.1 copy-start.3
  88.0 126.9 %all-gather.13.cloned.1.call-start = ((), (), s32[]{:S(2)}) async-start(), calls=%async_computation.2 | async-start | bytes 2359296 | tf_op jit(solution)/shard_map/all_gather | solution.py:33
  157.6 1.3 copy-start.1
  193.1 21.8 %copy-start.4 = (f32[2,64,2048]{2,1,0:T(8,128)S(1)}, f32[2,64,2048]{2,1,0:T(8,128)}, u32[]{:S(2)}) copy-start(f32[2,64,2048]{2,1,0:T(8,128)} %param.17) | copy-start | bytes 3145732
  290.8 2.8 copy-start.2
Sparse Core Ops, SparseCore 0:
  38.1 28.0 all-gather.8
  68.6 27.7 all-gather.10
  98.3 29.4 all-gather.14
  190.4 24.4 all-gather.12
